TPU v7x, 32 devices: a whole 2x2x4 slice. The times are simulated.
32 devices in a mesh: seq: 16 (over z, y, core), tensor: 2 (over x).
Axes of the slice: x: 2, y: 2, z: 4, core: 2. Of those that a mesh axis runs over, the one named last changes fastest.
Arguments:
- hidden: bfloat16 [1024, 7168], P('seq', 'tensor'), may hold values from -200 to 200
- attn_gain: float32 [7168], P('tensor'), may hold values from 0.25 to 1.75
- kv_down: bfloat16 [7168, 576], P('tensor'), may hold values from -0.0625 to 0.0625
- kv_gain: float32 [512], replicated, may hold values from 0.25 to 1.75
- q_nope: bfloat16 [1024, 16384], P('seq', 'tensor'), may hold values from -90 to 90
- q_pe: bfloat16 [1024, 8192], P('seq', 'tensor'), may hold values from -6 to 6
- w_uk: bfloat16 [128, 128, 512], P('tensor'), may hold values from -0.5 to 0.5
- w_uv: bfloat16 [128, 512, 128], P('tensor'), may hold values from -1 to 1
- doc_ids: int32 [1024], replicated, may hold values from 0 to 3, never falling along the last dimension, each value on 1 to 768 neighbouring positions
- slot_table: int32 [64], replicated, may hold values from 0 to 63, each once
Outputs:
- attn_values: bfloat16 [1024, 16384], P('seq', 'tensor')
- latent_cache: bfloat16 [1024, 576], P('seq')
Inputs may be any that keep to these rules, and one draw needn't show every extreme that they name: `doc_ids`: 4 documents packed in order, the longest exactly 768 tokens. `slot_table`: each cache slot receives exactly one token block.
All inputs are finite; a program needn't handle non-finite values.
Results may differ from a plain program's by a relative error of at most 0.0093.
Values may be sent and summed in bfloat16 or wider, within the bound.
A program may use at most 128 MiB of HBM per device.

v0:
```python
import math

import jax
import jax.numpy as jnp
from jax import lax
from jax.sharding import PartitionSpec as P

D = 7168
LATENT = 512
ROPE = 64
NOPE = 128
VD = 128
BLOCK = 16


EPSILON = 1e-06
MASKED = -1e30


def block_rows(total_rows):
    block_size = min(total_rows, 512)
    while total_rows % block_size:
        block_size -= 1
    return block_size


def angles(positions, width):
    middle = width // 2
    frequency = jnp.exp(jnp.arange(middle, dtype=jnp.float32) * (-2.0 * math.log(10000.0) / width))
    angle_table = positions[:, None] * frequency[None, :]
    return (jnp.cos(angle_table), jnp.sin(angle_table))


def rotate(values, cosine_part, sine_part):
    middle = values.shape[-1] // 2
    first_half = values[..., :middle]
    second_half = values[..., middle:]
    return jnp.concatenate(
        [
            first_half * cosine_part - second_half * sine_part,
            second_half * cosine_part + first_half * sine_part,
        ],
        axis=-1,
    )


def finish(projected, squares, positions, kv_gain):
    scaled = projected * lax.rsqrt(squares / D + EPSILON)[:, None]
    raw_latent = scaled[:, :LATENT]
    raw_key = scaled[:, LATENT:]
    latent = (
        raw_latent
        * lax.rsqrt(jnp.mean(raw_latent * raw_latent, axis=1, keepdims=True) + EPSILON)
        * kv_gain
    ).astype(jnp.bfloat16)
    cosine_part, sine_part = angles(positions.astype(jnp.float32), raw_key.shape[1])
    return (latent, rotate(raw_key, cosine_part, sine_part).astype(jnp.bfloat16))


def attend_keys(softmax_state, latent_keys, rope_keys, offset, queries):
    query_latent, query_rope, query_position, query_docs, doc_ids = queries
    key_count = latent_keys.shape[0]
    block_size = block_rows(key_count)
    needed = jnp.clip((query_position[-1] - offset) // block_size + 1, 0, key_count // block_size)

    def step(block_index, running):
        running_max, denominator, weighted = running
        start_row = block_index * block_size
        latent_block = lax.dynamic_slice_in_dim(latent_keys, start_row, block_size, 0)
        rope_block = lax.dynamic_slice_in_dim(rope_keys, start_row, block_size, 0)
        key_position = offset + start_row + jnp.arange(block_size, dtype=jnp.int32)
        key_docs = lax.dynamic_slice_in_dim(doc_ids, offset + start_row, block_size, 0)
        scores = jnp.einsum(
            "thc,uc->thu", query_latent, latent_block, preferred_element_type=jnp.float32
        )
        scores = scores + jnp.einsum(
            "thr,ur->thu", query_rope, rope_block, preferred_element_type=jnp.float32
        )
        scores = scores * (NOPE + ROPE) ** (-0.5)
        allowed = (
            (key_position[None, :] <= query_position[:, None])
            & (key_docs[None, :] == query_docs[:, None])
        )[:, None, :]
        scores = jnp.where(allowed, scores, MASKED)
        new_max = jnp.maximum(running_max, jnp.max(scores, axis=2))
        weights = jnp.where(allowed, jnp.exp(scores - new_max[:, :, None]), 0.0)
        factor = jnp.exp(running_max - new_max)
        denominator = denominator * factor + jnp.sum(weights, axis=2)
        weighted = weighted * factor[:, :, None] + jnp.einsum(
            "thu,uc->thc",
            weights.astype(jnp.bfloat16),
            latent_block,
            preferred_element_type=jnp.float32,
        )
        return (new_max, denominator, weighted)

    return lax.fori_loop(0, needed, step, softmax_state)


def place_rows(latent_keys, rope_keys, slot_table, first_row, row_count):
    key_count = latent_keys.shape[0]
    positions = jnp.arange(key_count, dtype=jnp.int32)
    targets = jnp.take(slot_table, positions // BLOCK)
    local_row = targets * BLOCK + positions % BLOCK - first_row
    selector = (local_row[None, :] == jnp.arange(row_count, dtype=jnp.int32)[:, None]).astype(
        jnp.bfloat16
    )
    return jnp.concatenate(
        [
            jnp.dot(selector, latent_keys, preferred_element_type=jnp.float32),
            jnp.dot(selector, rope_keys, preferred_element_type=jnp.float32),
        ],
        axis=1,
    )


def local(hidden, attn_gain, kv_down, kv_gain, q_nope, q_pe, w_uk, w_uv, doc_ids, slot_table):
    row_count = hidden.shape[0]
    head_count = w_uk.shape[0]
    first_row = lax.axis_index("seq") * row_count
    widened = hidden.astype(jnp.float32)
    squares = jnp.sum(widened * widened, axis=1)
    normed_in = (widened * attn_gain).astype(jnp.bfloat16)
    partial_projection = jnp.dot(normed_in, kv_down, preferred_element_type=jnp.float32)
    own_positions = first_row + jnp.arange(row_count, dtype=jnp.int32)
    projected, norm_sums = lax.psum((partial_projection, squares), "tensor")
    own_latent, own_rope = finish(projected, norm_sums, own_positions, kv_gain)
    cosine_part, sine_part = angles(own_positions.astype(jnp.float32), ROPE)
    query_rope = rotate(
        q_pe.astype(jnp.float32).reshape(row_count, head_count, ROPE),
        cosine_part[:, None, :],
        sine_part[:, None, :],
    ).astype(jnp.bfloat16)
    query_latent = jnp.einsum(
        "thd,hdc->thc",
        q_nope.reshape(row_count, head_count, NOPE),
        w_uk,
        preferred_element_type=jnp.float32,
    ).astype(jnp.bfloat16)
    query_docs = lax.dynamic_slice_in_dim(doc_ids, first_row, row_count, 0)
    queries = (query_latent, query_rope, own_positions, query_docs, doc_ids)
    softmax_state = (
        jnp.full((row_count, head_count), MASKED, jnp.float32),
        jnp.zeros((row_count, head_count), jnp.float32),
        jnp.zeros((row_count, head_count, LATENT), jnp.float32),
    )
    all_latent, all_rope = (
        lax.all_gather(own_latent, "seq", axis=0, tiled=True),
        lax.all_gather(own_rope, "seq", axis=0, tiled=True),
    )
    softmax_state = attend_keys(softmax_state, all_latent, all_rope, 0, queries)
    latent_cache = place_rows(all_latent, all_rope, slot_table, first_row, row_count)
    running_max, denominator, weighted = softmax_state
    mixed = (weighted / denominator[:, :, None]).astype(jnp.bfloat16)
    attn_values = jnp.einsum(
        "thc,hcv->thv", mixed, w_uv, preferred_element_type=jnp.float32
    ).astype(jnp.bfloat16)
    return (attn_values.reshape(row_count, head_count * VD), latent_cache.astype(jnp.bfloat16))


def solution(mesh):
    placed = (
        P("seq", "tensor"),
        P("tensor"),
        P("tensor", None),
        P(),
        P("seq", "tensor"),
        P("seq", "tensor"),
        P("tensor", None, None),
        P("tensor", None, None),
        P(),
        P(),
    )
    return jax.shard_map(
        local,
        mesh=mesh,
        in_specs=placed,
        out_specs=(P("seq", "tensor"), P("seq", None)),
        check_vma=False,
    )
```

profile of v0, /device:TPU:25, one launch (start us, length us, event | category | flops | bytes accessed | tf_op | source)
XLA Modules:
  0.0 156.9 jit_solution(14152977411204392782)
XLA Ops:
  7.2 4.4 %fusion.34 = f32[64,576]{1,0:T(8,128)} fusion(bf16[3584,576]{0,1:T(8,128)(2,1)} %param.14, bf16[64,3584]{1,0:T(8,128)(2,1)} %param.12, f32[3584]{0:T(1024)} %param.13), kind=kOutput, calls=%fused_computation.44 | convolution fusion | flops 264929280 | bytes 4749312 | tf_op jit(solution)/shard_map/dot_general | solution.py:124
  11.7 1.2 fusion.33
  17.0 4.2 %psum.15 = f32[64]{0:T(128)S(1)} all-reduce(f32[64]{0:T(128)S(1)} %fusion.33), channel_id=1, replica_groups=mesh['seq'=16,'tensor'=2] {'tensor'}, use_global_device_ids=true, to_apply=%region_2.0 | all-reduce | flops 64 | bytes 512 | tf_op jit(solution)/shard_map/psum | solution.py:126
  21.9 1.9 %reshape.223 = f32[64,64,64]{2,1,0:T(8,128)S(1)} reshape(bf16[64,4096]{1,0:T(8,128)(2,1)} %param.17) | data formatting | bytes 1572864 | tf_op jit(solution)/shard_map/reshape | solution.py:130
  23.9 4.6 %convert_bitcast_fusion = bf16[64,64,512]{2,0,1:T(8,128)(2,1)S(1)} fusion(bf16[64,128,512]{2,1,0:T(8,128)(2,1)} %param.18, bf16[64,8192]{1,0:T(8,128)(2,1)S(1)} %copy-done), kind=kOutput, calls=%fused_computation.29 | convolution fusion | flops 538968064 | bytes 13631488 | tf_op jit(solution)/shard_map/thd,hdc->thc/dot_general | solution.py:134
  28.5 4.3 %copy.17 = bf16[64,64,512]{2,1,0:T(8,128)(2,1)} copy(bf16[64,64,512]{2,0,1:T(8,128)(2,1)S(1)} %convert_bitcast_fusion) | data formatting | bytes 8388608
  33.4 0.9 all-reduce.2.cloned.1.call-done
  34.3 1.0 broadcast_multiply_fusion
  35.4 0.7 multiply_convert_fusion
  36.2 0.7 fusion.57
  36.9 0.7 fusion.56
  37.6 4.4 %compare_select_fusion.1 = s32[1024,1]{0,1:T(1,128)S(1)} fusion(s32[]{:T(128)} %bitcast.60, s32[]{:T(128)} %bitcast.61, s32[]{:T(128)} %bitcast.62, s32[]{:T(128)} %bitcast.63, s32[]{:T(128)} %bitcast.64, s32[]{:T(128)} %bitcast.66, s32[]{:T(128)} %bitcast.65), kind=kLoop, calls=%fused_computation.116 | loop fusion | flops 23552 | bytes 4124 | tf_op jit(solution)/shard_map/jit(_take)/gather | solution.py:103
  42.0 0.7 fusion.54
  42.7 0.7 fusion.55
  43.4 35.6 %fusion.46 = s32[1024]{0:T(1024)S(1)} fusion(pred[1024]{0:T(1024)(128)(4,1)S(1)} %compare_reduce_fusion, pred[1024]{0:T(1024)(128)(4,1)S(1)} %compare_reduce_fusion.1, pred[1024]{0:T(1024)(128)(4,1)S(1)} %compare_reduce_fusion.2, pred[1024]{0:T(1024)(128)(4,1)S(1)} %compare_reduce_fusion.3, pred[1024]{0:T(1024)(128)(4,1)S(1)} %compare_reduce_fusion.4, ...), kind=kLoop, calls=%fused_computation.138 | loop fusion | flops 80896 | bytes 66792 | tf_op jit(solution)/shard_map/sub | solution.py:104
  79.3 18.5 %all_gather.7 = bf16[1024,64]{1,0:T(8,128)(2,1)S(1)} all-gather(bf16[64,64]{1,0:T(8,128)(2,1)S(1)} %pad_maximum_fusion.2), channel_id=1, replica_groups=mesh['seq'=16,'tensor'=2] {'seq'}, dimensions={0}, use_global_device_ids=true | all-gather | bytes 139264 | tf_op jit(solution)/shard_map/all_gather | solution.py:149
  97.9 0.8 subtract_convert_fusion
  98.7 0.6 pad_maximum_fusion
  99.6 4.3 %broadcast_in_dim.39 = f32[64,64,512]{2,1,0:T(8,128)} broadcast(f32[]{:T(128)} %constant.89.clone.1), dimensions={} | broadcast | bytes 8388612 | tf_op jit(solution)/shard_map/broadcast_in_dim | solution.py:145
  103.9 31.3 %while.15 = (s32[]{:T(128)}, f32[64,64]{1,0:T(8,128)S(1)}, f32[64,64]{1,0:T(8,128)S(1)}, f32[64,64,512]{2,1,0:T(8,128)}, s32[]{:T(128)}, /*index=5*/s32[1024]{0:...) while((s32[]{:T(128)}, f32[64,64]{1,0:T(8,128)S(1)}, ...), condition=%wide.region_7.8_spmd.clone, body=%wide.region_4.7_spmd.clone.sunk | while | flops 4588675584 | bytes 65514460 | solution.py:97
  104.1 4.6 %fusion.79 = f32[512,64,64]{0,2,1:T(8,128)S(1)} fusion(bf16[64,64,512]{2,1,0:T(8,128)(2,1)} %get-tuple-element.342, bf16[1024,512]{1,0:T(8,128)(2,1)S(1)} %get-tuple-element.341, s32[]{:T(128)S(6)} %select_n.372), kind=kOutput, calls=%fused_computation.11.clone.1 | convolution fusion | flops 2147483648 | bytes 13107204 | tf_op jit(solution)/shard_map/while/body/thc,uc->thu/dot_general | solution.py:73
  108.6 1.5 fusion.80
  110.2 2.4 %fusion.81 = f32[64,64]{1,0:T(8,128)S(1)} fusion(f32[64,64,512]{2,1,0:T(8,128)S(1)} %get-tuple-element.299, f32[64,64]{1,0:T(8,128)S(1)} %max.10, pred[64,512]{1,0:T(8,128)(4,1)S(1)} %compare_and_fusion.2), kind=kLoop, calls=%fused_computation.5.clone.1 | loop fusion | flops 6287360 | bytes 8454144 | tf_op jit(solution)/shard_map/while/body/reduce_sum | solution.py:88
  112.6 7.0 %multiply_add_fusion.5 = f32[64,64,512]{2,1,0:T(8,128)} fusion(f32[64,64,512]{2,1,0:T(8,128)} %get-tuple-element.321, f32[64,64]{1,0:T(8,128)S(1)} %get-tuple-element.301, f32[64,64,512]{2,1,0:T(8,128)S(1)} %get-tuple-element.299, f32[64,64]{1,0:T(8,128)S(1)} %max.10, pred[64,512]{1,0:T(8,128)(4,1)S(1)} %compare_and_fusion.2, ...), kind=kOutput, calls=%fused_computation.2.clone.1 | convolution fusion | flops 2157969408 | bytes 25788420 | tf_op jit(solution)/shard_map/while/body/thu,uc->thc/dot_general | solution.py:89
  119.8 4.6 %fusion.79 = f32[512,64,64]{0,2,1:T(8,128)S(1)} fusion(bf16[64,64,512]{2,1,0:T(8,128)(2,1)} %get-tuple-element.342, bf16[1024,512]{1,0:T(8,128)(2,1)S(1)} %get-tuple-element.341, s32[]{:T(128)S(6)} %select_n.372), kind=kOutput, calls=%fused_computation.11.clone.1 | convolution fusion | flops 2147483648 | bytes 13107204 | tf_op jit(solution)/shard_map/while/body/thc,uc->thu/dot_general | solution.py:73
  124.3 1.5 fusion.80
  125.9 2.4 %fusion.81 = f32[64,64]{1,0:T(8,128)S(1)} fusion(f32[64,64,512]{2,1,0:T(8,128)S(1)} %get-tuple-element.299, f32[64,64]{1,0:T(8,128)S(1)} %max.10, pred[64,512]{1,0:T(8,128)(4,1)S(1)} %compare_and_fusion.2), kind=kLoop, calls=%fused_computation.5.clone.1 | loop fusion | flops 6287360 | bytes 8454144 | tf_op jit(solution)/shard_map/while/body/reduce_sum | solution.py:88
  128.3 6.9 %multiply_add_fusion.5 = f32[64,64,512]{2,1,0:T(8,128)} fusion(f32[64,64,512]{2,1,0:T(8,128)} %get-tuple-element.321, f32[64,64]{1,0:T(8,128)S(1)} %get-tuple-element.301, f32[64,64,512]{2,1,0:T(8,128)S(1)} %get-tuple-element.299, f32[64,64]{1,0:T(8,128)S(1)} %max.10, pred[64,512]{1,0:T(8,128)(4,1)S(1)} %compare_and_fusion.2, ...), kind=kOutput, calls=%fused_computation.2.clone.1 | convolution fusion | flops 2157969408 | bytes 25788420 | tf_op jit(solution)/shard_map/while/body/thu,uc->thc/dot_general | solution.py:89
  135.2 3.9 %divide_convert_fusion = bf16[64,64,512]{2,1,0:T(8,128)(2,1)S(1)} fusion(f32[64,64,512]{2,1,0:T(8,128)} %get-tuple-element.66, f32[64,64]{1,0:T(8,128)S(1)} %get-tuple-element.67), kind=kLoop, calls=%fused_computation.26 | loop fusion | flops 4194304 | bytes 12599296 | tf_op jit(solution)/shard_map/convert_element_type | solution.py:154
  139.2 8.8 %fusion.27 = bf16[64,8,8,128]{3,2,1,0:T(8,128)(2,1)S(1)} fusion(bf16[64,512,128]{2,1,0:T(8,128)(2,1)} %param.19, bf16[64,64,512]{2,1,0:T(8,128)(2,1)S(1)} %divide_convert_fusion), kind=kOutput, calls=%fused_computation.33 | convolution fusion | flops 537395200 | bytes 13631488 | tf_op jit(solution)/shard_map/thc,hcv->thv/dot_general | solution.py:155
  148.0 1.2 copy.34
  149.5 0.6 pad_maximum_fusion.1
  (103 shorter events, 4.2 us)
Async XLA Ops:
  7.2 16.7 %copy-start = (bf16[64,8192]{1,0:T(8,128)(2,1)S(1)}, bf16[64,8192]{1,0:T(8,128)(2,1)}, u32[]{:S(2)}) copy-start(bf16[64,8192]{1,0:T(8,128)(2,1)} %param.16) | copy-start | bytes 3145732
  7.2 27.1 %all-reduce.2.cloned.1.call-start = ((), (), s32[]{:S(2)}) async-start(), calls=%async_computation | async-start | bytes 327680 | tf_op jit(solution)/shard_map/psum | solution.py:126
  11.7 87.9 %all-gather.2.cloned.1.call-start = ((), (), s32[]{:S(2)}) async-start(), calls=%async_computation.1 | async-start | bytes 1114112 | tf_op jit(solution)/shard_map/all_gather | solution.py:148
  23.9 9.0 %copy-start.4 = (s32[1024]{0:T(1024)S(1)}, s32[1024]{0:T(1024)}, u32[]{:S(2)}) copy-start(s32[1024]{0:T(1024)} %param.20) | copy-start | bytes 12292
  23.9 11.6 %copy-start.5 = (f32[512]{0:T(512)S(1)}, f32[512]{0:T(512)}, u32[]{:S(2)}) copy-start(f32[512]{0:T(512)} %param.15) | copy-start | bytes 6148
  23.9 12.3 %copy-start.3 = (s32[64]{0:T(128)S(1)}, s32[64]{0:T(128)}, u32[]{:S(2)}) copy-start(s32[64]{0:T(128)} %param.21) | copy-start | bytes 772
  99.5 4.3 %copy-start.2 = (bf16[1024,512]{1,0:T(8,128)(2,1)S(1)}, bf16[1024,512]{1,0:T(8,128)(2,1)}, u32[]{:S(2)}) copy-start(bf16[1024,512]{1,0:T(8,128)(2,1)} %all-gather.2.cloned.1.call-done) | copy-start | bytes 3145732
  135.2 14.9 %copy-start.1 = (bf16[64,8192]{1,0:T(8,128)(2,1)S(1)}, bf16[64,8192]{1,0:T(8,128)(2,1)}, u32[]{:S(2)}) copy-start(bf16[64,8192]{1,0:T(8,128)(2,1)} %param.16) | copy-start | bytes 3145732
Sparse Core Ops, SparseCore 0:
  11.8 22.4 all-reduce.1
  37.0 37.7 all-gather.1
where the time goes:
time: 158 us; the launch traced here: 157 us
  other arithmetic  56.2 us (36%)
  matrix products  44.4 us (28%)
  blocking collectives  22.6 us (14%)
  between operations  16.9 us (11%)
  local copies, waits for them, and re-layouts  15.6 us (10%)
    sub x1, other arithmetic, place_rows(): local_row = targets * BLOCK + positions % BLOCK - first_row  35.6 us
    all_gather x1, blocking collectives, local(): lax.all_gather(own_rope, 'seq', axis=0, tiled=True)  18.5 us
    dot_general x2, matrix products, step(): jnp.einsum('thu,uc->thc', weights.astype(jnp.bfloat16), latent_block, pre...  13.9 us
    dot_general x2, matrix products, step(): jnp.einsum('thc,uc->thu', query_latent, latent_block, preferred_element_t...  9.14 us
    dot_general x1, matrix products, local(): jnp.einsum('thc,hcv->thv', mixed, w_uv, preferred_element_type=jnp.float32)  8.85 us
    gather x58, other arithmetic, place_rows(): targets = jnp.take(slot_table, positions // BLOCK)  6.31 us
    reduce_sum x2, other arithmetic, step(): denominator = denominator * factor + jnp.sum(weights, axis=2)  4.73 us
    dot_general x1, matrix products, local(): jnp.einsum('thd,hdc->thc', q_nope.reshape(row_count, head_count, NOPE), w...  4.65 us
  transfers between devices with their start and end apart: 2, of which 1 were waited for; matrix products, arithmetic and copies ran while one was open for 38% of the time, Pallas kernels for 0%

commit v1 on v0

v1 whole, which is shorter than its diff:
```python
import functools
import math

import jax
import jax.numpy as jnp
import numpy as np
from jax import lax
from jax.experimental import pallas as pl
from jax.experimental.pallas import tpu as pltpu
from jax.sharding import PartitionSpec as P

LATENT = 512
ROPE = 64
NOPE = 128
VD = 128
BLOCK = 16
LANES = 128
EPSILON = 1e-06
MASKED = -1e30
WIDE = LATENT + 2 * ROPE
VMEM_BYTES = 56 * 1024 * 1024
MESH = pl.DeviceIdType.MESH


def rope_table(tokens):
    middle = ROPE // 2
    frequency = np.exp(np.arange(middle, dtype=np.float32) * np.float32(-2.0 * math.log(10000.0) / ROPE)).astype(np.float32)
    angle = (np.arange(tokens, dtype=np.float32)[:, None] * frequency[None, :]).astype(np.float32)
    cosine, sine = np.cos(angle), np.sin(angle)
    return np.concatenate([cosine] * 4 + [-sine, sine, -sine, sine], axis=1).astype(np.float32)


def rotate_pair(values, cosine, sine, lane):
    half = ROPE // 2
    swapped = jnp.where(
        lane % ROPE < half,
        pltpu.roll(values, LANES - half, 1),
        pltpu.roll(values, half, 1),
    )
    return values * cosine + swapped * sine


def gather_kernel(
    nseq, width,
    hidden, gain, kv_down, kv_gain, q_nope, q_pe, w_uk, table,
    qc_out, kv_out,
    hidden_v, gain_v, down_v, kv_gain_v, nope_v, pe_v, uk_v, table_v,
    partial, incoming, kv, qc,
    in_sem, down_sem, uk_sem, out_sem, x_send, x_recv, send_sem, recv_sem,
):
    rows, model = hidden_v.shape
    heads = uk_v.shape[0]
    half = rows // 2
    groups = nseq // 4
    me = lax.axis_index("seq")
    side = lax.axis_index("tensor")
    far = me // 4
    place = lax.rem(me, 4)
    ybit = place // 2
    core = lax.rem(place, 2)

    first_row = pl.multiple_of(me * rows, rows)
    early = [
        pltpu.make_async_copy(hidden, hidden_v, in_sem.at[0]),
        pltpu.make_async_copy(gain, gain_v, in_sem.at[1]),
        pltpu.make_async_copy(kv_gain, kv_gain_v, in_sem.at[2]),
        pltpu.make_async_copy(table.at[pl.ds(first_row, rows)], table_v, in_sem.at[3]),
    ]
    for copy in early[:2]:
        copy.start()
    chunks = down_sem.shape[0]
    depth = model // chunks
    down_copies = []
    for i in range(chunks):
        part = pl.ds(i * depth, depth)
        down_copies.append(pltpu.make_async_copy(kv_down.at[part], down_v.at[part], down_sem.at[i]))
        down_copies[-1].start()
    for copy in early[2:]:
        copy.start()
    query_copies = [
        pltpu.make_async_copy(q_nope, nope_v, in_sem.at[4]),
        pltpu.make_async_copy(q_pe, pe_v, in_sem.at[5]),
    ]
    for copy in query_copies:
        copy.start()
    stages = uk_sem.shape[0]
    stage_heads = heads // stages
    uk_copies = []
    for i in range(stages):
        part = pl.ds(i * stage_heads, stage_heads)
        uk_copies.append(pltpu.make_async_copy(w_uk.at[part], uk_v.at[part], uk_sem.at[i]))
        uk_copies[-1].start()

    def peer(seq, tensor):
        return {"seq": seq, "tensor": tensor}

    def seq_of(group, y, c):
        return group * 4 + y * 2 + c

    x_peer = peer(me, 1 - side)
    y_peer = peer(seq_of(far, 1 - ybit, core), side)
    core_peer = peer(seq_of(far, ybit, 1 - core), side)
    z_groups = [lax.rem(far + k, groups) for k in range(1, groups)]
    z_peers = [peer(seq_of(g, ybit, core), side) for g in z_groups]

    barrier = pltpu.get_barrier_semaphore()
    everyone = [x_peer, y_peer, core_peer] + z_peers
    for target in everyone:
        pl.semaphore_signal(barrier, inc=1, device_id=target, device_id_type=MESH)

    for copy in early[:2]:
        copy.wait()
    squares = jnp.zeros((rows, 1), jnp.float32)
    total = jnp.zeros((rows, width), jnp.float32)
    for i in range(chunks):
        part = pl.ds(i * depth, depth)
        widened = hidden_v[:, part].astype(jnp.float32)
        squares = squares + jnp.sum(widened * widened, axis=1, keepdims=True)
        normed = (widened * gain_v[:, part]).astype(jnp.bfloat16)
        down_copies[i].wait()
        total = total + jnp.dot(normed, down_v[part, :], preferred_element_type=jnp.float32)
    partial[:, pl.ds(0, width)] = total
    partial[:, pl.ds(width, WIDE - width)] = jnp.broadcast_to(squares, (rows, WIDE - width))
    pl.semaphore_wait(barrier, len(everyone))
    theirs = pl.multiple_of((1 - side) * half, half)
    ours = pl.multiple_of(side * half, half)
    x_copy = pltpu.make_async_remote_copy(
        src_ref=partial.at[pl.ds(theirs, half)],
        dst_ref=incoming,
        send_sem=x_send.at[0],
        recv_sem=x_recv.at[0],
        device_id=x_peer,
        device_id_type=MESH,
    )
    x_copy.start()

    lane = lax.broadcasted_iota(jnp.int32, (1, LANES), 1)
    for copy in early[2:] + query_copies:
        copy.wait()
    out_copies = []

    def queries(stage):
        uk_copies[stage].wait()

        def pair(index, carry):
            head = index * 2
            at = pl.multiple_of(index * LANES, LANES)
            turned = rotate_pair(
                pe_v[:, pl.ds(at, LANES)].astype(jnp.float32),
                table_v[:, :LANES], table_v[:, LANES:], lane,
            )
            for j in range(2):
                column = pl.multiple_of((head + j) * NOPE, NOPE)
                qc[head + j, :, pl.ds(0, LATENT)] = jnp.dot(
                    nope_v[:, pl.ds(column, NOPE)], uk_v[head + j],
                    preferred_element_type=jnp.float32,
                ).astype(jnp.bfloat16)
                mine = (lane < ROPE) if j == 0 else (lane >= ROPE)
                qc[head + j, :, pl.ds(LATENT, LANES)] = jnp.where(mine, turned, 0.0).astype(jnp.bfloat16)
            return carry

        lax.fori_loop(stage * stage_heads // 2, (stage + 1) * stage_heads // 2, pair, 0, unroll=2)
        part = pl.ds(stage * stage_heads, stage_heads)
        copy = pltpu.make_async_copy(qc.at[part], qc_out.at[part], out_sem.at[stage])
        copy.start()
        out_copies.append(copy)

    queries(0)
    queries(1)

    x_copy.wait()
    summed = partial[pl.ds(ours, half), :] + incoming[...]
    norm = lax.rsqrt(summed[:, width:width + 1] / (2 * model) + EPSILON)
    raw = summed[:, :LATENT] * norm
    mean = jnp.sum(raw * raw, axis=1, keepdims=True) * (1.0 / LATENT)
    latent = raw * lax.rsqrt(mean + EPSILON) * kv_gain_v[...]
    tail = summed[:, LATENT:] * norm
    doubled = jnp.where(lane < ROPE, tail, pltpu.roll(tail, ROPE, 1))
    turned = rotate_pair(
        doubled, table_v[pl.ds(ours, half), :LANES], table_v[pl.ds(ours, half), LANES:], lane
    )

    def rows_of(seq, tensor):
        return pl.ds(pl.multiple_of(seq * rows + tensor * half, half), half)

    own = rows_of(me, side)
    kv[own, pl.ds(0, LATENT)] = latent.astype(jnp.bfloat16)
    kv[own, pl.ds(LATENT, LANES)] = turned.astype(jnp.bfloat16)

    sent = []

    def chunk(seq, tensor):
        return seq * 2 + tensor

    def send(seq, tensor, target):
        span = rows_of(seq, tensor)
        copy = pltpu.make_async_remote_copy(
            src_ref=kv.at[span],
            dst_ref=kv.at[span],
            send_sem=send_sem.at[len(sent)],
            recv_sem=recv_sem.at[chunk(seq, tensor)],
            device_id=target,
            device_id_type=MESH,
        )
        copy.start()
        sent.append(copy)

    def arrive(seq, tensor):
        span = rows_of(seq, tensor)
        pltpu.make_async_remote_copy(
            src_ref=kv.at[span],
            dst_ref=kv.at[span],
            send_sem=send_sem.at[0],
            recv_sem=recv_sem.at[chunk(seq, tensor)],
            device_id=x_peer,
            device_id_type=MESH,
        ).wait_recv()

    for target in z_peers:
        send(me, side, target)
    send(me, side, x_peer)
    send(me, side, y_peer)
    send(me, side, core_peer)
    queries(2)
    for g in z_groups:
        s = seq_of(g, ybit, core)
        arrive(s, side)
        send(s, side, x_peer)
        send(s, side, y_peer)
        send(s, side, core_peer)
    queries(3)
    for k in range(groups):
        g = lax.rem(far + k, groups)
        s = seq_of(g, ybit, core)
        arrive(s, 1 - side)
        if k % 2 == 0:
            send(s, 1 - side, y_peer)
        send(s, 1 - side, core_peer)
        s = seq_of(g, 1 - ybit, core)
        arrive(s, side)
        if k % 2 == 1:
            send(s, side, x_peer)
        send(s, side, core_peer)
    for k in range(groups):
        s = seq_of(lax.rem(far + k, groups), 1 - ybit, core)
        arrive(s, 1 - side)
        send(s, 1 - side, core_peer)
    for k in range(groups):
        g = lax.rem(far + k, groups)
        for y in range(2):
            for t in range(2):
                arrive(seq_of(g, y, 1 - core), t)
    last = pltpu.make_async_copy(kv, kv_out, out_sem.at[stages])
    last.start()
    for copy in sent:
        copy.wait_send()
    for copy in out_copies:
        copy.wait()
    last.wait()


def attend_kernel(sub, slots, qc, uv, kv, docs, out, cache, bias):
    heads, rows, _ = qc.shape
    tokens = kv.shape[0]
    me = lax.axis_index("seq")
    first_row = me * rows

    @pl.when(pl.program_id(0) == 0)
    def _():
        key = lax.broadcasted_iota(jnp.int32, (rows, tokens), 1)
        query = first_row + lax.broadcasted_iota(jnp.int32, (rows, tokens), 0)
        key_doc = jnp.broadcast_to(docs[...], (rows, tokens))
        query_doc = jnp.sum(
            jnp.where(key == query, key_doc, 0).astype(jnp.float32), axis=1, keepdims=True
        )
        allowed = (key <= query) & (key_doc.astype(jnp.float32) == query_doc)
        bias[...] = jnp.where(allowed, 0.0, MASKED)
        per = rows // BLOCK

        def place(block, carry):
            slot = slots[block]

            @pl.when(slot // per == me)
            def _():
                to = pl.ds(pl.multiple_of(lax.rem(slot, per) * BLOCK, BLOCK), BLOCK)
                source = pl.ds(pl.multiple_of(block * BLOCK, BLOCK), BLOCK)
                cache[to, :] = kv[source, pl.ds(0, cache.shape[1])]

            return carry

        lax.fori_loop(0, tokens // BLOCK, place, 0)

    scale = (NOPE + ROPE) ** (-0.5) * math.log2(math.e)
    for start in range(0, heads, sub):
        query = qc[pl.ds(start, sub)].reshape(sub * rows, WIDE)
        scores = lax.dot_general(
            query, kv[...], (((1,), (1,)), ((), ())), preferred_element_type=jnp.float32
        )
        scores = (scores.reshape(sub, rows, tokens) + bias[...][None]).reshape(sub * rows, tokens)
        top = jnp.max(scores, axis=1, keepdims=True)
        weights = jnp.exp2((scores - top) * scale)
        denominator = jnp.sum(weights, axis=1, keepdims=True)
        mixed = jnp.dot(
            weights.astype(jnp.bfloat16), kv[:, pl.ds(0, LATENT)], preferred_element_type=jnp.float32
        )
        mixed = (mixed / denominator).astype(jnp.bfloat16)
        for j in range(sub):
            out[:, pl.ds((start + j) * VD, VD)] = jnp.dot(
                mixed[j * rows:(j + 1) * rows], uv[start + j], preferred_element_type=jnp.float32
            ).astype(jnp.bfloat16)


def local(nseq, hidden, attn_gain, kv_down, kv_gain, q_nope, q_pe, w_uk, w_uv, doc_ids, slot_table):
    rows, model = hidden.shape
    width = kv_down.shape[1]
    heads = w_uk.shape[0]
    tokens = doc_ids.shape[0]
    table = jnp.asarray(rope_table(tokens))
    stages = 4
    anywhere = pl.BlockSpec(memory_space=pl.ANY)
    dma = pltpu.SemaphoreType.DMA
    groups = nseq // 4
    sends = (groups + 2) + (groups - 1) * 3 + groups * 3 + groups
    qc, kv = pl.pallas_call(
        functools.partial(gather_kernel, nseq, width),
        out_shape=(
            jax.ShapeDtypeStruct((heads, rows, WIDE), jnp.bfloat16),
            jax.ShapeDtypeStruct((tokens, WIDE), jnp.bfloat16),
        ),
        in_specs=[anywhere] * 8,
        out_specs=(anywhere, anywhere),
        scratch_shapes=[
            pltpu.VMEM((rows, model), jnp.bfloat16),
            pltpu.VMEM((1, model), jnp.float32),
            pltpu.VMEM((model, width), jnp.bfloat16),
            pltpu.VMEM((1, LATENT), jnp.float32),
            pltpu.VMEM((rows, heads * NOPE), jnp.bfloat16),
            pltpu.VMEM((rows, heads * ROPE), jnp.bfloat16),
            pltpu.VMEM((heads, NOPE, LATENT), jnp.bfloat16),
            pltpu.VMEM((rows, 2 * LANES), jnp.float32),
            pltpu.VMEM((rows, WIDE), jnp.float32),
            pltpu.VMEM((rows // 2, WIDE), jnp.float32),
            pltpu.VMEM((tokens, WIDE), jnp.bfloat16),
            pltpu.VMEM((heads, rows, WIDE), jnp.bfloat16),
            dma((6,)),
            dma((7,)),
            dma((stages,)),
            dma((stages + 1,)),
            dma((1,)),
            dma((1,)),
            dma((sends,)),
            dma((2 * nseq,)),
        ],
        compiler_params=pltpu.CompilerParams(
            collective_id=0, has_side_effects=True, vmem_limit_bytes=VMEM_BYTES
        ),
        name="gather",
    )(
        hidden, attn_gain.reshape(1, model), kv_down, kv_gain.reshape(1, LATENT),
        q_nope, q_pe, w_uk, table,
    )
    group = 8
    return pl.pallas_call(
        functools.partial(attend_kernel, 4),
        out_shape=(
            jax.ShapeDtypeStruct((rows, heads * VD), jnp.bfloat16),
            jax.ShapeDtypeStruct((rows, width), jnp.bfloat16),
        ),
        grid_spec=pltpu.PrefetchScalarGridSpec(
            num_scalar_prefetch=1,
            grid=(heads // group,),
            in_specs=[
                pl.BlockSpec((group, rows, WIDE), lambda i, s: (i, 0, 0)),
                pl.BlockSpec((group, LATENT, VD), lambda i, s: (i, 0, 0)),
                pl.BlockSpec((tokens, WIDE), lambda i, s: (0, 0)),
                pl.BlockSpec((1, tokens), lambda i, s: (0, 0)),
            ],
            out_specs=[
                pl.BlockSpec((rows, group * VD), lambda i, s: (0, i)),
                pl.BlockSpec((rows, width), lambda i, s: (0, 0)),
            ],
            scratch_shapes=[pltpu.VMEM((rows, tokens), jnp.float32)],
        ),
        compiler_params=pltpu.CompilerParams(
            dimension_semantics=("arbitrary",), vmem_limit_bytes=VMEM_BYTES
        ),
        name="attend",
    )(slot_table, qc, w_uv, kv, doc_ids.reshape(1, tokens))


def solution(mesh):
    placed = (
        P("seq", "tensor"),
        P("tensor"),
        P("tensor", None),
        P(),
        P("seq", "tensor"),
        P("seq", "tensor"),
        P("tensor", None, None),
        P("tensor", None, None),
        P(),
        P(),
    )
    return jax.shard_map(
        functools.partial(local, mesh.shape["seq"]),
        mesh=mesh,
        in_specs=placed,
        out_specs=(P("seq", "tensor"), P("seq", None)),
        check_vma=False,
    )
```

time: 158 us -> 57.5 us (0.36)
  the two profiles are of different devices: /device:TPU:25 before, /device:TPU:1 now
where the time goes in v1:
time: 57.5 us; the launch traced here: 57.2 us
  Pallas kernels  48.7 us (85%)
  local copies, waits for them, and re-layouts  7.86 us (14%)
  between operations  0.64 us (1%)
    pallas_call x1, Pallas kernels, local(): pl.pallas_call(functools.partial(gather_kernel, nseq, width), out_shape=(...  24.9 us
    pallas_call x1, Pallas kernels, local(): pl.pallas_call(functools.partial(attend_kernel, 4), out_shape=(jax.ShapeD...  23.8 us
    unnamed x1, local copies, waits for them, and re-layouts  6.54 us
    reshape x1, local copies, waits for them, and re-layouts, local(): attn_gain.reshape(1, model)  1.33 us

profile of v1, /device:TPU:1, one launch (start us, length us, event | category | flops | bytes accessed | tf_op | source)
XLA Modules:
  0.0 57.2 jit_solution(8220181817512129171)
XLA Ops:
  0.6 1.3 %reshape.13.gain = f32[1,3584]{1,0:T(1,128)} reshape(f32[3584]{0:T(1024)} %param.12) | data formatting | bytes 28672 | tf_op jit(solution)/shard_map/reshape | solution.py:359
  2.0 6.5 %copy.13.kv_down = bf16[3584,576]{1,0:T(8,128)(2,1)} copy(bf16[3584,576]{0,1:T(8,128)(2,1)} %param.13) | data formatting | bytes 8257536 | tf_op args[2]
  8.5 24.9 %gather.1 = (bf16[64,64,640]{2,1,0:T(8,128)(2,1)}, bf16[1024,640]{1,0:T(8,128)(2,1)}) custom-call(bf16[64,3584]{1,0:T(8,128)(2,1)} %hidden.1, f32[1,3584]{1,0:T(1,128)} %reshape.13.gain, bf16[3584,576]{1,0:T(8,128)(2,1)} %copy.13.kv_down, f32[1,512]{1,0:T(1,128)} %bitcast.3, bf16[64,8192]{1,0:T(8,128)(2,1)} %q_nope.1, bf16[64,4096]{1,0:T(8,128)(2,1)} %q_pe.1, ...), custom_call_target="tpu_custom_call" | custom-call | tf_op jit(solution)/shard_map/gather/pallas_call | solution.py:324
  33.4 23.8 %attend.1 = (bf16[64,8192]{1,0:T(8,128)(2,1)}, bf16[64,576]{1,0:T(8,128)(2,1)}) custom-call(s32[64]{0:T(128)} %slots.1, bf16[64,64,640]{2,1,0:T(8,128)(2,1)} %get-tuple-element.4.qc, bf16[64,512,128]{2,1,0:T(8,128)(2,1)} %uv.1, bf16[1024,640]{1,0:T(8,128)(2,1)} %get-tuple-element.5.kv, s32[1,1024]{1,0:T(1,128)} %bitcast.2), custom_call_target="tpu_custom_call" | custom-call | tf_op jit(solution)/shard_map/attend/pallas_call | solution.py:363

commit v2 on v1

--- a/solution.py
+++ b/solution.py
@@ -20,6 +20,9 @@
 WIDE = LATENT + 2 * ROPE
 VMEM_BYTES = 56 * 1024 * 1024
 MESH = pl.DeviceIdType.MESH
+WINDOWS = (2, 4, 6, 7, 8)
+GROUP = 8
+SUB = 4
 
 
 def rope_table(tokens):
@@ -73,7 +76,9 @@
     down_copies = []
     for i in range(chunks):
         part = pl.ds(i * depth, depth)
-        down_copies.append(pltpu.make_async_copy(kv_down.at[part], down_v.at[part], down_sem.at[i]))
+        down_copies.append(
+            pltpu.make_async_copy(kv_down.at[:, part], down_v.at[:, part], down_sem.at[i])
+        )
         down_copies[-1].start()
     for copy in early[2:]:
         copy.start()
@@ -100,7 +105,11 @@
     x_peer = peer(me, 1 - side)
     y_peer = peer(seq_of(far, 1 - ybit, core), side)
     core_peer = peer(seq_of(far, ybit, 1 - core), side)
-    z_groups = [lax.rem(far + k, groups) for k in range(1, groups)]
+    upper = far // ((groups + 1) // 2)
+    step = 1 - 2 * upper
+    inward = far + upper * (groups - 1 - 2 * far)
+    hops = [1, 2 + inward, 3 - inward] if groups == 4 else list(range(1, groups))
+    z_groups = [lax.rem(far + step * hop + groups, groups) for hop in hops]
     z_peers = [peer(seq_of(g, ybit, core), side) for g in z_groups]
 
     barrier = pltpu.get_barrier_semaphore()
@@ -116,9 +125,11 @@
         part = pl.ds(i * depth, depth)
         widened = hidden_v[:, part].astype(jnp.float32)
         squares = squares + jnp.sum(widened * widened, axis=1, keepdims=True)
-        normed = (widened * gain_v[:, part]).astype(jnp.bfloat16)
+        normed = (widened * gain_v[part].reshape(1, depth)).astype(jnp.bfloat16)
         down_copies[i].wait()
-        total = total + jnp.dot(normed, down_v[part, :], preferred_element_type=jnp.float32)
+        total = total + lax.dot_general(
+            normed, down_v[:, part], (((1,), (1,)), ((), ())), preferred_element_type=jnp.float32
+        )
     partial[:, pl.ds(0, width)] = total
     partial[:, pl.ds(width, WIDE - width)] = jnp.broadcast_to(squares, (rows, WIDE - width))
     pl.semaphore_wait(barrier, len(everyone))
@@ -229,8 +240,7 @@
         send(s, side, y_peer)
         send(s, side, core_peer)
     queries(3)
-    for k in range(groups):
-        g = lax.rem(far + k, groups)
+    for k, g in enumerate([far] + z_groups):
         s = seq_of(g, ybit, core)
         arrive(s, 1 - side)
         if k % 2 == 0:
@@ -241,12 +251,11 @@
         if k % 2 == 1:
             send(s, side, x_peer)
         send(s, side, core_peer)
-    for k in range(groups):
-        s = seq_of(lax.rem(far + k, groups), 1 - ybit, core)
+    for g in [far] + z_groups:
+        s = seq_of(g, 1 - ybit, core)
         arrive(s, 1 - side)
         send(s, 1 - side, core_peer)
-    for k in range(groups):
-        g = lax.rem(far + k, groups)
+    for g in [far] + z_groups:
         for y in range(2):
             for t in range(2):
                 arrive(seq_of(g, y, 1 - core), t)
@@ -259,21 +268,36 @@
     last.wait()
 
 
-def attend_kernel(sub, slots, qc, uv, kv, docs, out, cache, bias):
+def attend_kernel(sub, slots, qc, uv, kv, docs, out, cache, bias, bounds):
     heads, rows, _ = qc.shape
     tokens = kv.shape[0]
     me = lax.axis_index("seq")
     first_row = me * rows
+    sizes = [tokens * n // 8 for n in WINDOWS]
 
     @pl.when(pl.program_id(0) == 0)
     def _():
-        key = lax.broadcasted_iota(jnp.int32, (rows, tokens), 1)
-        query = first_row + lax.broadcasted_iota(jnp.int32, (rows, tokens), 0)
-        key_doc = jnp.broadcast_to(docs[...], (rows, tokens))
-        query_doc = jnp.sum(
-            jnp.where(key == query, key_doc, 0).astype(jnp.float32), axis=1, keepdims=True
-        )
-        allowed = (key <= query) & (key_doc.astype(jnp.float32) == query_doc)
+        key = lax.broadcasted_iota(jnp.int32, (1, tokens), 1)
+        first_doc = jnp.sum(jnp.where(key == first_row, docs[...], 0).astype(jnp.float32), axis=1, keepdims=True)
+        start = jnp.sum((docs[...].astype(jnp.float32) < first_doc).astype(jnp.float32)).astype(jnp.int32)
+        needed = first_row + rows - start
+        choice = jnp.int32(0)
+        size = jnp.int32(sizes[0])
+        for i in range(1, len(sizes)):
+            more = needed > sizes[i - 1]
+            choice = jnp.where(more, i, choice)
+            size = jnp.where(more, sizes[i], size)
+        window = jnp.maximum(first_row + rows - size, 0)
+        bounds[0] = choice
+        bounds[1] = window
+        wide = (rows, tokens)
+        at = lax.broadcasted_iota(jnp.int32, wide, 1)
+        query = first_row + lax.broadcasted_iota(jnp.int32, wide, 0)
+        every_doc = jnp.broadcast_to(docs[...].astype(jnp.float32), wide)
+        query_doc = jnp.sum(jnp.where(at == query, every_doc, 0.0), axis=1, keepdims=True)
+        lowest = jnp.sum((every_doc < query_doc).astype(jnp.float32), axis=1, keepdims=True)
+        position = window + at
+        allowed = (position <= query) & (position.astype(jnp.float32) >= lowest)
         bias[...] = jnp.where(allowed, 0.0, MASKED)
         per = rows // BLOCK
 
@@ -291,23 +315,38 @@
         lax.fori_loop(0, tokens // BLOCK, place, 0)
 
     scale = (NOPE + ROPE) ** (-0.5) * math.log2(math.e)
-    for start in range(0, heads, sub):
-        query = qc[pl.ds(start, sub)].reshape(sub * rows, WIDE)
-        scores = lax.dot_general(
-            query, kv[...], (((1,), (1,)), ((), ())), preferred_element_type=jnp.float32
-        )
-        scores = (scores.reshape(sub, rows, tokens) + bias[...][None]).reshape(sub * rows, tokens)
-        top = jnp.max(scores, axis=1, keepdims=True)
-        weights = jnp.exp2((scores - top) * scale)
-        denominator = jnp.sum(weights, axis=1, keepdims=True)
-        mixed = jnp.dot(
-            weights.astype(jnp.bfloat16), kv[:, pl.ds(0, LATENT)], preferred_element_type=jnp.float32
-        )
-        mixed = (mixed / denominator).astype(jnp.bfloat16)
-        for j in range(sub):
-            out[:, pl.ds((start + j) * VD, VD)] = jnp.dot(
-                mixed[j * rows:(j + 1) * rows], uv[start + j], preferred_element_type=jnp.float32
-            ).astype(jnp.bfloat16)
+    window = pl.multiple_of(bounds[1], rows)
+
+    def attend(size):
+        span = pl.ds(window, size)
+
+        def score(start):
+            query = qc[pl.ds(start, sub)].reshape(sub * rows, WIDE)
+            return lax.dot_general(
+                query, kv[span, :], (((1,), (1,)), ((), ())), preferred_element_type=jnp.float32
+            )
+
+        scores = score(0)
+        for start in range(0, heads, sub):
+            following = score(start + sub) if start + sub < heads else None
+            scores = (scores.reshape(sub, rows, size) + bias[:, :size][None]).reshape(sub * rows, size)
+            top = jnp.max(scores, axis=1, keepdims=True)
+            weights = jnp.exp2((scores - top) * scale)
+            denominator = jnp.sum(weights, axis=1, keepdims=True)
+            mixed = jnp.dot(
+                weights.astype(jnp.bfloat16), kv[span, pl.ds(0, LATENT)], preferred_element_type=jnp.float32
+            )
+            mixed = (mixed / denominator).astype(jnp.bfloat16)
+            for j in range(sub):
+                out[:, pl.ds((start + j) * VD, VD)] = jnp.dot(
+                    mixed[j * rows:(j + 1) * rows], uv[start + j], preferred_element_type=jnp.float32
+                ).astype(jnp.bfloat16)
+            scores = following
+
+    for i, size in enumerate(sizes):
+        @pl.when(bounds[0] == i)
+        def _(size=size):
+            attend(size)
 
 
 def local(nseq, hidden, attn_gain, kv_down, kv_gain, q_nope, q_pe, w_uk, w_uv, doc_ids, slot_table):
@@ -331,8 +370,8 @@
         out_specs=(anywhere, anywhere),
         scratch_shapes=[
             pltpu.VMEM((rows, model), jnp.bfloat16),
-            pltpu.VMEM((1, model), jnp.float32),
-            pltpu.VMEM((model, width), jnp.bfloat16),
+            pltpu.VMEM((model,), jnp.float32),
+            pltpu.VMEM((width, model), jnp.bfloat16),
             pltpu.VMEM((1, LATENT), jnp.float32),
             pltpu.VMEM((rows, heads * NOPE), jnp.bfloat16),
             pltpu.VMEM((rows, heads * ROPE), jnp.bfloat16),
@@ -356,12 +395,12 @@
         ),
         name="gather",
     )(
-        hidden, attn_gain.reshape(1, model), kv_down, kv_gain.reshape(1, LATENT),
+        hidden, attn_gain, kv_down.T, kv_gain.reshape(1, LATENT),
         q_nope, q_pe, w_uk, table,
     )
-    group = 8
+    group = GROUP
     return pl.pallas_call(
-        functools.partial(attend_kernel, 4),
+        functools.partial(attend_kernel, SUB),
         out_shape=(
             jax.ShapeDtypeStruct((rows, heads * VD), jnp.bfloat16),
             jax.ShapeDtypeStruct((rows, width), jnp.bfloat16),
@@ -379,7 +418,7 @@
                 pl.BlockSpec((rows, group * VD), lambda i, s: (0, i)),
                 pl.BlockSpec((rows, width), lambda i, s: (0, 0)),
             ],
-            scratch_shapes=[pltpu.VMEM((rows, tokens), jnp.float32)],
+            scratch_shapes=[pltpu.VMEM((rows, tokens), jnp.float32), pltpu.SMEM((2,), jnp.int32)],
         ),
         compiler_params=pltpu.CompilerParams(
             dimension_semantics=("arbitrary",), vmem_limit_bytes=VMEM_BYTES

time: 57.5 us -> 42.8 us (0.74)
  local copies, waits for them, and re-layouts: 7.86 us -> 0 us
  Pallas kernels: 48.7 us -> 41.3 us
    pallas_call x1, Pallas kernels: 23.8 us -> 14.7 us  [local(): pl.pallas_call(functools.partial(attend_kernel, SUB), out_shape=(jax.Shap...]
    unnamed x1 -> x0, local copies, waits for them, and re-layouts: 6.54 us -> none
    pallas_call x1, Pallas kernels: 24.9 us -> 26.7 us  [local(): pl.pallas_call(functools.partial(gather_kernel, nseq, width), out_shape=(...]
    reshape x1 -> x0, local copies, waits for them, and re-layouts: 1.33 us -> none  [local(): attn_gain.reshape(1, model)]
where the time goes in v2:
time: 42.8 us; the launch traced here: 42 us
  Pallas kernels  41.3 us (96%)
  between operations  0.64 us (1%)
    pallas_call x1, Pallas kernels, local(): pl.pallas_call(functools.partial(gather_kernel, nseq, width), out_shape=(...  26.7 us
    pallas_call x1, Pallas kernels, local(): pl.pallas_call(functools.partial(attend_kernel, SUB), out_shape=(jax.Shap...  14.7 us

profile of v2, /device:TPU:1, one launch (start us, length us, event | category | flops | bytes accessed | tf_op | source)
XLA Modules:
  0.0 42.0 jit_solution(16521411157348660354)
XLA Ops:
  0.6 26.7 %gather.1 = (bf16[64,64,640]{2,1,0:T(8,128)(2,1)}, bf16[1024,640]{1,0:T(8,128)(2,1)}) custom-call(bf16[64,3584]{1,0:T(8,128)(2,1)} %hidden.1, f32[3584]{0:T(1024)} %gain.1, bf16[576,3584]{1,0:T(8,128)(2,1)} %bitcast.3, f32[1,512]{1,0:T(1,128)} %bitcast.5, bf16[64,8192]{1,0:T(8,128)(2,1)} %q_nope.1, bf16[64,4096]{1,0:T(8,128)(2,1)} %q_pe.1, ...), custom_call_target="tpu_custom_call" | custom-call | tf_op jit(solution)/shard_map/gather/pallas_call | solution.py:363
  27.3 14.7 %attend.1 = (bf16[64,8192]{1,0:T(8,128)(2,1)}, bf16[64,576]{1,0:T(8,128)(2,1)}) custom-call(s32[64]{0:T(128)} %slots.1, bf16[64,64,640]{2,1,0:T(8,128)(2,1)} %get-tuple-element.4.qc, bf16[64,512,128]{2,1,0:T(8,128)(2,1)} %uv.1, bf16[1024,640]{1,0:T(8,128)(2,1)} %get-tuple-element.5.kv, s32[1,1024]{1,0:T(1,128)} %bitcast.4), custom_call_target="tpu_custom_call" | custom-call | tf_op jit(solution)/shard_map/attend/pallas_call | solution.py:402
